TPU v7x, 32 devices: a whole 2x2x4 slice. The times are simulated.
32 devices in a mesh: ens: 2 (over y), box: 4 (over z), slab: 4 (over x, core).
Axes of the slice: x: 2, y: 2, z: 4, core: 2. Of those that a mesh axis runs over, the one named last changes fastest.
Arguments:
- pressure_now: float32 [4, 64, 64, 256], P('ens', 'box', 'slab'), parts along dimension 0, may hold values from -6 to 6
- pressure_prev: float32 [4, 64, 64, 256], P('ens', 'box', 'slab'), parts along dimension 0, may hold values from -6 to 6
- courant_sq: float32 [64, 64, 256], P('box', 'slab'), may hold values from 0.04 to 0.28
- member_profiles: float32 [8, 64], replicated, may hold values from -0.15 to 0.15
- member_ids: int32 [4], P('ens'), parts along dimension 0, may hold values from 0 to 7, as said below
- stored_slabs: float32 [8, 16, 6144], P('slab'), may hold values from -6 to 6
- slab_home: int32 [2], P('ens'), parts along dimension 0, may hold values from 0 to 7
- interp_weights: float32 [2, 16], replicated, may hold values from -1.5 to 1.5
- surface_cells: int32 [6, 1024], replicated, may hold values from 0 to 1048575, as said below
Outputs:
- pressure_next: float32 [4, 64, 64, 256], P('ens', 'box', 'slab'), parts along dimension 0
- pressure_last: float32 [4, 64, 64, 256], P('ens', 'box', 'slab'), parts along dimension 0
There are 2 independent parts, one for each index of `ens`. A program takes and returns all parts, laid end to end along the dimension named above; an argument that names none is the same for every part. Nothing has to cross between parts.
Inputs may be any that keep to these rules, and one draw needn't show every extreme that they name: `surface_cells`: row f lists 1024 cells, flat index (x 64 + z) * 256 + y, on one face of the box surface 0 cells inside the grid: x low, x high, z low, z high, y low, y high in this order; the other two coordinates lie on the surface; on every face other than the two depth faces, every depth of the surface occurs; cells may repeat. `slab_home`: block k is stored on the slab device k // 2, in its slot k % 2. `member_ids`: the members' profiles are all different.
All inputs are finite; a program needn't handle non-finite values.
Results may differ from a plain program's by a relative error of at most 0.000098.
Values sent between devices are 32-bit elements; how exact they have to be, the bound alone decides.
No kernel may reach another device: no remote copies, remote signals or barrier semaphores. Data moves between devices by JAX's collectives and lax.ppermute only.
A program may use at most 64 MiB of HBM per device.

v0:
```python
import jax
import jax.numpy as jnp
from jax import lax
from jax.sharding import PartitionSpec as P


def extended(array, sides, width):
    for axis, dim in sides:
        peers, length = (lax.axis_size(axis), array.shape[dim])
        up = [(i, (i + 1) % peers) for i in range(peers - 1)]
        down = [(j, i) for i, j in up]
        last = lax.slice_in_dim(array, length - width, length, axis=dim)
        leading = lax.slice_in_dim(array, 0, width, axis=dim)
        before = lax.ppermute(last, axis, up)
        after = lax.ppermute(leading, axis, down)
        array = jnp.concatenate([before, array, after], axis=dim)
    return array


def laplace(ext):
    inner = ext[:, 1:-1, 1:-1, :]
    beside = ext[:, 2:, 1:-1, :] + ext[:, :-2, 1:-1, :]
    beside = beside + ext[:, 1:-1, 2:, :] + ext[:, 1:-1, :-2, :]
    padded = jnp.pad(inner, ((0, 0), (0, 0), (0, 0), (1, 1)))
    beside = beside + padded[:, :, :, 2:] + padded[:, :, :, :-2]
    return beside - 6.0 * inner


def inject(field, cells, point_values, anchor_x, anchor_z, total_z):
    extent_x, extent_z, depth_y = (field.shape[1], field.shape[2], field.shape[3])
    plane = total_z * depth_y
    cell_x = cells // plane
    remain = cells % plane
    cell_z = remain // depth_y
    cell_y = remain % depth_y
    local_x = cell_x - anchor_x
    local_z = cell_z - anchor_z
    inside = (local_x >= 0) & (local_x < extent_x) & (local_z >= 0) & (local_z < extent_z)
    volume = extent_x * extent_z * depth_y
    target = jnp.where(inside, (local_x * extent_z + local_z) * depth_y + cell_y, volume)
    source = jnp.zeros((volume,), jnp.float32).at[target].add(point_values, mode="drop")
    return field + source.reshape(extent_x, extent_z, depth_y)[None]


def on_device(
    pressure_now,
    pressure_prev,
    courant_sq,
    member_profiles,
    member_ids,
    stored_slabs,
    slab_home,
    interp_weights,
    surface_cells,
):
    members, width_x, width_z, depth_y = pressure_now.shape
    total_z = width_z * lax.axis_size("slab")
    start_x = lax.axis_index("box") * width_x
    start_z = lax.axis_index("slab") * width_z
    profiles = member_profiles.shape[0]
    choose = (member_ids[:, None] == jnp.arange(profiles, dtype=jnp.int32)[None, :]).astype(
        jnp.float32
    )
    profile_all = jnp.dot(choose, member_profiles, precision=lax.Precision.HIGHEST)
    profile_here = lax.dynamic_slice_in_dim(profile_all, start_z, width_z, 1)
    coef = courant_sq[None] * (1.0 + profile_here[:, None, :, None])
    slots = stored_slabs.shape[0]
    home = slab_home[0]
    is_owner = lax.axis_index("slab") == home // slots
    mine = lax.dynamic_index_in_dim(stored_slabs, home % slots, 0, keepdims=False)
    partial_values = jnp.dot(interp_weights, mine, precision=lax.Precision.HIGHEST)
    offered = jnp.where(is_owner, partial_values, jnp.zeros_like(partial_values))
    values = lax.psum(offered, "slab")
    cells = surface_cells.reshape(-1)
    count = interp_weights.shape[0]
    prev, now = (pressure_prev, pressure_now)
    for step in range(count):
        ext = extended(now, (("box", 1), ("slab", 2)), 1)
        nxt = 2.0 * now - prev + coef * laplace(ext)
        nxt = inject(nxt, cells, values[step], start_x, start_z, total_z)
        prev, now = (now, nxt)
    return (now, prev)


def solution(mesh):
    in_specs = (
        P("ens", "box", "slab", None),
        P("ens", "box", "slab", None),
        P("box", "slab", None),
        P(),
        P("ens"),
        P("slab", None, None),
        P("ens"),
        P(),
        P(),
    )
    out_specs = (P("ens", "box", "slab", None), P("ens", "box", "slab", None))
    return jax.shard_map(
        on_device, mesh=mesh, in_specs=in_specs, out_specs=out_specs, check_vma=False
    )
```

profile of v0, /device:TPU:1, one launch (start us, length us, event | category | flops | bytes accessed | tf_op | source)
XLA Modules:
  0.0 109.3 jit_solution(6065750017297019400)
XLA Ops:
  0.6 0.0 copy-start
  0.6 0.0 copy-start.1
  0.7 0.9 fusion.31
  1.5 4.0 %collective-permute-start.1 = (f32[2,1,16,256]{3,2,1,0:T(8,128)S(1)}, f32[2,1,16,256]{3,2,1,0:T(8,128)S(1)}, u32[]{:S(2)}, u32[]{:S(2)}) collective-permute-start(f32[2,1,16,256]{3,2,1,0:T(8,128)S(1)} %get-tuple-element.9), channel_id=1, source_target_pairs={{0,4},{4,8},{8,12},{1,5},{5,9},{9,13},{2,6},{6,10},{10,14},{3,7},{... | collective-permute-start | bytes 98312 | tf_op jit(solution)/shard_map/ppermute | solution.py:14
  5.6 1.3 %collective-permute-start = (f32[2,1,16,256]{3,2,1,0:T(8,128)S(1)}, f32[2,1,16,256]{3,2,1,0:T(8,128)S(1)}, u32[]{:S(2)}, u32[]{:S(2)}) collective-permute-start(f32[2,1,16,256]{3,2,1,0:T(8,128)S(1)} %get-tuple-element.8), channel_id=1, source_target_pairs={{4,0},{8,4},{12,8},{5,1},{9,5},{13,9},{6,2},{10,6},{14,10},{7,3},{... | collective-permute-start | bytes 98312 | tf_op jit(solution)/shard_map/ppermute | solution.py:15
  7.5 0.0 copy-done
  7.5 1.0 fusion
  8.6 11.0 %psum.7 = f32[2,6144]{1,0:T(2,128)S(1)} all-reduce(f32[2,6144]{1,0:T(2,128)S(1)} %fusion), channel_id=1, replica_groups=mesh['ens'=2,'box'=4,'slab'=4] {'slab'}, use_global_device_ids=true, to_apply=%region_0.1 | all-reduce | flops 12288 | bytes 98304 | tf_op jit(solution)/shard_map/psum | solution.py:73
  19.6 0.0 copy-start.6
  19.6 0.6 fusion.32
  20.2 0.1 copy-done.6
  20.4 0.0 copy-start.8
  20.4 0.0 copy-start.9
  20.4 0.4 compare_select_fusion
  20.8 0.2 copy-done.8
  21.1 0.0 copy-done.9
  21.1 0.0 copy-start.7
  21.1 0.2 fusion.24
  21.2 0.0 collective-permute-done.1
  21.3 0.0 copy-done.1
  21.3 0.0 copy-start.4
  21.3 0.0 collective-permute-done
  21.3 0.1 fusion.29
  21.4 3.1 %collective-permute-start.2 = (f32[2,18,1,256]{3,2,1,0:T(1,128)S(1)}, f32[2,18,1,256]{3,2,1,0:T(1,128)S(1)}, u32[]{:S(2)}, u32[]{:S(2)}) collective-permute-start(f32[2,18,1,256]{3,2,1,0:T(1,128)S(1)} %get-tuple-element.4), channel_id=1, source_target_pairs={{1,0},{2,1},{3,2},{5,4},{6,5},{7,6},{9,8},{10,9},{11,10},{13,12},{... | collective-permute-start | bytes 110600 | tf_op jit(solution)/shard_map/ppermute | solution.py:15
  24.5 2.6 %collective-permute-start.3 = (f32[2,18,1,256]{3,2,1,0:T(1,128)S(1)}, f32[2,18,1,256]{3,2,1,0:T(1,128)}, u32[]{:S(2)}, u32[]{:S(2)}) collective-permute-start(f32[2,18,1,256]{3,2,1,0:T(1,128)S(1)} %get-tuple-element.5), channel_id=1, source_target_pairs={{0,1},{1,2},{2,3},{4,5},{5,6},{6,7},{8,9},{9,10},{10,11},{12,13},{... | collective-permute-start | bytes 110600 | tf_op jit(solution)/shard_map/ppermute | solution.py:14
  27.2 0.1 dynamic-slice_add_fusion
  27.2 0.0 copy-done.7
  27.2 32.6 %scatter_custom_fusion = f32[65536]{0:T(1024)S(1)} fusion(s32[6144]{0:T(1024)S(1)} %bitcast.21, f32[6144]{0:T(1024)S(1)} %bitcast.24, f32[]{:T(128)} %constant.98.clone.1), kind=kCustom, calls=%fused_computation.43 | custom fusion | flops 6144 | bytes 262148 | tf_op jit(solution)/shard_map/scatter-add | solution.py:41
  59.9 0.0 copy-start.3
  59.9 0.1 add.178
  60.0 0.0 collective-permute-done.2
  60.0 0.0 copy-start.5
  60.0 0.6 copy-done.5
  60.6 0.0 collective-permute-done.3
  60.6 0.0 copy-done.4
  60.6 0.2 copy-done.3
  60.8 1.2 %fusion.2 = f32[2,16,16,256]{3,2,1,0:T(8,128)S(1)} fusion(f32[2,16,16,256]{3,2,1,0:T(8,128)S(1)} %copy-done.1, f32[2,18,16,256]{3,2,1,0:T(8,128)S(1)} %constant_dynamic-update-slice_fusion, f32[2,18,1,256]{3,2,1,0:T(1,128)} %collective-permute-done.3, f32[2,18,1,256]{3,2,1,0:T(1,128)} %copy-done.5, f32[2,1,16,256]{3,2,1,0:T(8,128)S(1)} %collective-permute-done.1, ...), kind=kLoop, calls=%fused_computation.11 | loop fusion | flops 2228224 | bytes 2826368 | tf_op jit(solution)/shard_map/add | solution.py:42
  62.0 0.0 copy-start.2
  62.1 1.3 %collective-permute-start.4 = (f32[2,1,16,256]{3,2,1,0:T(8,128)S(1)}, f32[2,1,16,256]{3,2,1,0:T(8,128)S(1)}, u32[]{:S(2)}, u32[]{:S(2)}) collective-permute-start(f32[2,1,16,256]{3,2,1,0:T(8,128)S(1)} %get-tuple-element.7), channel_id=1, source_target_pairs={{4,0},{8,4},{12,8},{5,1},{9,5},{13,9},{6,2},{10,6},{14,10},{7,3},{... | collective-permute-start | bytes 98312 | tf_op jit(solution)/shard_map/ppermute | solution.py:15
  63.4 5.2 %collective-permute-start.5 = (f32[2,1,16,256]{3,2,1,0:T(8,128)S(1)}, f32[2,1,16,256]{3,2,1,0:T(8,128)S(1)}, u32[]{:S(2)}, u32[]{:S(2)}) collective-permute-start(f32[2,1,16,256]{3,2,1,0:T(8,128)S(1)} %get-tuple-element.6), channel_id=1, source_target_pairs={{0,4},{4,8},{8,12},{1,5},{5,9},{9,13},{2,6},{6,10},{10,14},{3,7},{... | collective-permute-start | bytes 98312 | tf_op jit(solution)/shard_map/ppermute | solution.py:14
  68.5 0.0 collective-permute-done.4
  68.5 1.0 collective-permute-done.5
  69.5 0.1 pad_maximum_fusion.14
  69.6 2.6 %collective-permute-start.6 = (f32[2,18,1,256]{3,2,1,0:T(1,128)S(1)}, f32[2,18,1,256]{3,2,1,0:T(1,128)S(1)}, u32[]{:S(2)}, u32[]{:S(2)}) collective-permute-start(f32[2,18,1,256]{3,2,1,0:T(1,128)S(1)} %get-tuple-element.2), channel_id=1, source_target_pairs={{1,0},{2,1},{3,2},{5,4},{6,5},{7,6},{9,8},{10,9},{11,10},{13,12},{... | collective-permute-start | bytes 110600 | tf_op jit(solution)/shard_map/ppermute | solution.py:15
  72.2 3.0 %collective-permute-start.7 = (f32[2,18,1,256]{3,2,1,0:T(1,128)S(1)}, f32[2,18,1,256]{3,2,1,0:T(1,128)S(1)}, u32[]{:S(2)}, u32[]{:S(2)}) collective-permute-start(f32[2,18,1,256]{3,2,1,0:T(1,128)S(1)} %get-tuple-element.3), channel_id=1, source_target_pairs={{0,1},{1,2},{2,3},{4,5},{5,6},{6,7},{8,9},{9,10},{10,11},{12,13},{... | collective-permute-start | bytes 110600 | tf_op jit(solution)/shard_map/ppermute | solution.py:14
  75.2 32.8 %scatter_custom_fusion.1 = f32[65536]{0:T(1024)S(1)} fusion(s32[6144]{0:T(1024)} %bitcast.22, f32[6144]{0:T(1024)} %bitcast.23, f32[]{:T(128)} %constant.98.clone.1), kind=kCustom, calls=%fused_computation.41 | custom fusion | flops 6144 | bytes 262656 | tf_op jit(solution)/shard_map/scatter-add | solution.py:41
  107.9 0.1 add.187
  108.0 0.0 collective-permute-done.6
  108.0 0.0 collective-permute-done.7
  108.1 0.0 copy-done.2
  108.1 1.3 %fusion.4 = f32[2,16,16,256]{3,2,1,0:T(8,128)} fusion(f32[2,16,16,256]{3,2,1,0:T(8,128)S(1)} %fusion.2, f32[2,18,1,256]{3,2,1,0:T(1,128)S(1)} %collective-permute-done.7, f32[2,1,16,256]{3,2,1,0:T(8,128)S(1)} %collective-permute-done.4, f32[2,1,16,256]{3,2,1,0:T(8,128)S(1)} %collective-permute-done.5, f32[2,18,1,256]{3,2,1,0:T(1,128)S(1)} %collective-permute-done.6, ...), kind=kLoop, calls=%fused_computation.13 | loop fusion | flops 2752512 | bytes 2236544 | tf_op jit(solution)/shard_map/add | solution.py:42
  (5 shorter events, 0.1 us)
Async XLA Ops:
  0.6 6.9 %copy-start = (f32[2,16,6144]{2,1,0:T(8,128)S(1)}, f32[2,16,6144]{2,1,0:T(8,128)}, u32[]{:S(2)}) copy-start(f32[2,16,6144]{2,1,0:T(8,128)} %param.14) | copy-start | bytes 2359300
  0.6 20.6 %copy-start.1 = (f32[2,16,16,256]{3,2,1,0:T(8,128)S(1)}, f32[2,16,16,256]{3,2,1,0:T(8,128)}, u32[]{:S(2)}) copy-start(f32[2,16,16,256]{3,2,1,0:T(8,128)} %param.9) | copy-start | bytes 1572868
  1.5 19.7 %collective-permute-start.1 = (f32[2,1,16,256]{3,2,1,0:T(8,128)S(1)}, f32[2,1,16,256]{3,2,1,0:T(8,128)S(1)}, u32[]{:S(2)}, u32[]{:S(2)}) collective-permute-start(f32[2,1,16,256]{3,2,1,0:T(8,128)S(1)} %get-tuple-element.9), channel_id=1, source_target_pairs={{0,4},{4,8},{8,12},{1,5},{5,9},{9,13},{2,6},{6,10},{10,14},{3,7},{... | collective-permute-start | bytes 98312 | tf_op jit(solution)/shard_map/ppermute | solution.py:14
  5.6 15.8 %collective-permute-start = (f32[2,1,16,256]{3,2,1,0:T(8,128)S(1)}, f32[2,1,16,256]{3,2,1,0:T(8,128)S(1)}, u32[]{:S(2)}, u32[]{:S(2)}) collective-permute-start(f32[2,1,16,256]{3,2,1,0:T(8,128)S(1)} %get-tuple-element.8), channel_id=1, source_target_pairs={{4,0},{8,4},{12,8},{5,1},{9,5},{13,9},{6,2},{10,6},{14,10},{7,3},{... | collective-permute-start | bytes 98312 | tf_op jit(solution)/shard_map/ppermute | solution.py:15
  19.6 0.8 copy-start.6
  20.4 0.7 copy-start.8
  20.4 0.7 copy-start.9
  21.1 6.2 %copy-start.7 = (s32[6144,1]{0,1:T(1,128)}, s32[6144,1]{0,1:T(1,128)S(1)}, u32[]{:S(2)}) copy-start(s32[6144,1]{0,1:T(1,128)S(1)} %compare_select_fusion) | copy-start | bytes 73732
  21.3 39.3 %copy-start.4 = (f32[2,16,16,256]{3,2,1,0:T(8,128)S(1)}, f32[2,16,16,256]{3,2,1,0:T(8,128)}, u32[]{:S(2)}) copy-start(f32[2,16,16,256]{3,2,1,0:T(8,128)} %param.10) | copy-start | bytes 1572868
  21.4 38.6 %collective-permute-start.2 = (f32[2,18,1,256]{3,2,1,0:T(1,128)S(1)}, f32[2,18,1,256]{3,2,1,0:T(1,128)S(1)}, u32[]{:S(2)}, u32[]{:S(2)}) collective-permute-start(f32[2,18,1,256]{3,2,1,0:T(1,128)S(1)} %get-tuple-element.4), channel_id=1, source_target_pairs={{1,0},{2,1},{3,2},{5,4},{6,5},{7,6},{9,8},{10,9},{11,10},{13,12},{... | collective-permute-start | bytes 110600 | tf_op jit(solution)/shard_map/ppermute | solution.py:15
  24.5 36.1 %collective-permute-start.3 = (f32[2,18,1,256]{3,2,1,0:T(1,128)S(1)}, f32[2,18,1,256]{3,2,1,0:T(1,128)}, u32[]{:S(2)}, u32[]{:S(2)}) collective-permute-start(f32[2,18,1,256]{3,2,1,0:T(1,128)S(1)} %get-tuple-element.5), channel_id=1, source_target_pairs={{0,1},{1,2},{2,3},{4,5},{5,6},{6,7},{8,9},{9,10},{10,11},{12,13},{... | collective-permute-start | bytes 110600 | tf_op jit(solution)/shard_map/ppermute | solution.py:14
  59.9 1.0 copy-start.3
  60.0 0.6 copy-start.5
  62.0 46.0 %copy-start.2 = (f32[2,16,16,256]{3,2,1,0:T(8,128)}, f32[2,16,16,256]{3,2,1,0:T(8,128)S(1)}, u32[]{:S(2)}) copy-start(f32[2,16,16,256]{3,2,1,0:T(8,128)S(1)} %fusion.2) | copy-start | bytes 1572868
  62.1 6.5 %collective-permute-start.4 = (f32[2,1,16,256]{3,2,1,0:T(8,128)S(1)}, f32[2,1,16,256]{3,2,1,0:T(8,128)S(1)}, u32[]{:S(2)}, u32[]{:S(2)}) collective-permute-start(f32[2,1,16,256]{3,2,1,0:T(8,128)S(1)} %get-tuple-element.7), channel_id=1, source_target_pairs={{4,0},{8,4},{12,8},{5,1},{9,5},{13,9},{6,2},{10,6},{14,10},{7,3},{... | collective-permute-start | bytes 98312 | tf_op jit(solution)/shard_map/ppermute | solution.py:15
  63.4 6.2 %collective-permute-start.5 = (f32[2,1,16,256]{3,2,1,0:T(8,128)S(1)}, f32[2,1,16,256]{3,2,1,0:T(8,128)S(1)}, u32[]{:S(2)}, u32[]{:S(2)}) collective-permute-start(f32[2,1,16,256]{3,2,1,0:T(8,128)S(1)} %get-tuple-element.6), channel_id=1, source_target_pairs={{0,4},{4,8},{8,12},{1,5},{5,9},{9,13},{2,6},{6,10},{10,14},{3,7},{... | collective-permute-start | bytes 98312 | tf_op jit(solution)/shard_map/ppermute | solution.py:14
  69.6 38.4 %collective-permute-start.6 = (f32[2,18,1,256]{3,2,1,0:T(1,128)S(1)}, f32[2,18,1,256]{3,2,1,0:T(1,128)S(1)}, u32[]{:S(2)}, u32[]{:S(2)}) collective-permute-start(f32[2,18,1,256]{3,2,1,0:T(1,128)S(1)} %get-tuple-element.2), channel_id=1, source_target_pairs={{1,0},{2,1},{3,2},{5,4},{6,5},{7,6},{9,8},{10,9},{11,10},{13,12},{... | collective-permute-start | bytes 110600 | tf_op jit(solution)/shard_map/ppermute | solution.py:15
  72.2 35.8 %collective-permute-start.7 = (f32[2,18,1,256]{3,2,1,0:T(1,128)S(1)}, f32[2,18,1,256]{3,2,1,0:T(1,128)S(1)}, u32[]{:S(2)}, u32[]{:S(2)}) collective-permute-start(f32[2,18,1,256]{3,2,1,0:T(1,128)S(1)} %get-tuple-element.3), channel_id=1, source_target_pairs={{0,1},{1,2},{2,3},{4,5},{5,6},{6,7},{8,9},{9,10},{10,11},{12,13},{... | collective-permute-start | bytes 110600 | tf_op jit(solution)/shard_map/ppermute | solution.py:14
where the time goes:
time: 110 us; the launch traced here: 109 us
  other arithmetic  68.5 us (62%)
  starting transfers between devices  23.1 us (21%)
  blocking collectives  11 us (10%)
  local copies, waits for them, and re-layouts  3.01 us (3%)
  between operations  1.62 us (1%)
  matrix products  1.2 us (1%)
    scatter-add x2, other arithmetic, inject(): jnp.zeros((volume,), jnp.float32).at[target].add(point_values, mode='drop')  65.4 us
    ppermute x4, starting transfers between devices, extended(): before = lax.ppermute(last, axis, up)  14.8 us
    psum x1, blocking collectives, on_device(): values = lax.psum(offered, 'slab')  11 us
    ppermute x4, starting transfers between devices, extended(): after = lax.ppermute(leading, axis, down)  8.3 us
    add x2, other arithmetic, inject(): return field + source.reshape(extent_x, extent_z, depth_y)[None]  2.5 us
  transfers between devices with their start and end apart: 8, of which 1 were waited for; matrix products, arithmetic and copies ran while one was open for 62% of the time, Pallas kernels for 0%

commit v1 on v0

--- a/solution.py
+++ b/solution.py
@@ -70,7 +70,8 @@
     mine = lax.dynamic_index_in_dim(stored_slabs, home % slots, 0, keepdims=False)
     partial_values = jnp.dot(interp_weights, mine, precision=lax.Precision.HIGHEST)
     offered = jnp.where(is_owner, partial_values, jnp.zeros_like(partial_values))
-    values = lax.psum(offered, "slab")
+    terms = lax.all_gather(offered, "slab")
+    values = jnp.sum(terms, axis=0)
     cells = surface_cells.reshape(-1)
     count = interp_weights.shape[0]
     prev, now = (pressure_prev, pressure_now)

time: 110 us -> 105 us (0.955)
  blocking collectives: 11 us -> 6.52 us
    psum x1 -> x0, blocking collectives: 11 us -> none  [on_device(): values = lax.psum(offered, 'slab')]
    all_gather x0 -> x1, blocking collectives: none -> 6.52 us  [on_device(): terms = lax.all_gather(offered, 'slab')]
    ppermute x4, starting transfers between devices: 8.3 us -> 7.06 us  [extended(): after = lax.ppermute(leading, axis, down)]
  transfers between devices with their start and end apart: 8 -> 8, of which waited for: 1 -> 1; matrix products, arithmetic and copies ran while one was open for 62% -> 64% of each run, Pallas kernels for 0% -> 0%
where the time goes in v1:
time: 105 us
  other arithmetic  68.5 us (65%)
  starting transfers between devices  22.7 us (22%)
  blocking collectives  6.52 us (6%)
  local copies, waits for them, and re-layouts  3.64 us (3%)
  between operations  1.62 us (2%)
  waiting for transfers between devices  1.19 us (1%)
    scatter-add x2, other arithmetic, inject(): jnp.zeros((volume,), jnp.float32).at[target].add(point_values, mode='drop')  65.4 us
    ppermute x4, starting transfers between devices, extended(): before = lax.ppermute(last, axis, up)  15.7 us
    ppermute x4, starting transfers between devices, extended(): after = lax.ppermute(leading, axis, down)  7.06 us
    all_gather x1, blocking collectives, on_device(): terms = lax.all_gather(offered, 'slab')  6.52 us
    add x2, other arithmetic, inject(): return field + source.reshape(extent_x, extent_z, depth_y)[None]  2.5 us
  transfers between devices with their start and end apart: 8, of which 1 were waited for; matrix products, arithmetic and copies ran while one was open for 64% of the time, Pallas kernels for 0%

profile of v1, /device:TPU:1, one launch (start us, length us, event | category | flops | bytes accessed | tf_op | source)
XLA Modules:
  0.0 104.8 jit_solution(11898029093393558072)
XLA Ops:
  0.6 0.0 copy-start
  0.6 0.9 fusion.31
  1.5 4.0 %collective-permute-start.1 = (f32[2,1,16,256]{3,2,1,0:T(8,128)S(1)}, f32[2,1,16,256]{3,2,1,0:T(8,128)S(1)}, u32[]{:S(2)}, u32[]{:S(2)}) collective-permute-start(f32[2,1,16,256]{3,2,1,0:T(8,128)S(1)} %get-tuple-element.9), channel_id=1, source_target_pairs={{0,4},{4,8},{8,12},{1,5},{5,9},{9,13},{2,6},{6,10},{10,14},{3,7},{... | collective-permute-start | bytes 98312 | tf_op jit(solution)/shard_map/ppermute | solution.py:14
  5.5 1.3 %collective-permute-start = (f32[2,1,16,256]{3,2,1,0:T(8,128)S(1)}, f32[2,1,16,256]{3,2,1,0:T(8,128)S(1)}, u32[]{:S(2)}, u32[]{:S(2)}) collective-permute-start(f32[2,1,16,256]{3,2,1,0:T(8,128)S(1)} %get-tuple-element.8), channel_id=1, source_target_pairs={{4,0},{8,4},{12,8},{5,1},{9,5},{13,9},{6,2},{10,6},{14,10},{7,3},{... | collective-permute-start | bytes 98312 | tf_op jit(solution)/shard_map/ppermute | solution.py:15
  7.5 0.0 copy-start.8
  7.5 0.0 copy-done
  7.5 0.7 copy-done.8
  8.2 0.3 fusion
  8.5 0.0 copy-start.1
  8.5 6.5 %all-gather.1 = f32[4,2,6144]{2,1,0:T(2,128)S(1)} all-gather(f32[1,2,6144]{2,1,0:T(2,128)S(1)} %fusion), channel_id=2, replica_groups=mesh['ens'=2,'box'=4,'slab'=4] {'slab'}, dimensions={0}, use_global_device_ids=true | all-gather | bytes 245760 | tf_op jit(solution)/shard_map/all_gather | solution.py:73
  15.0 0.1 reduce_sum.9
  15.1 0.0 copy-start.6
  15.1 0.6 fusion.32
  15.8 0.1 copy-done.6
  15.9 0.0 copy-start.9
  15.9 0.0 copy-start.10
  15.9 0.4 compare_select_fusion
  16.4 0.2 copy-done.9
  16.6 0.0 copy-done.10
  16.6 0.0 copy-start.7
  16.6 0.2 fusion.24
  16.8 0.0 collective-permute-done.1
  16.8 0.0 copy-done.1
  16.9 0.0 copy-start.4
  16.9 0.0 collective-permute-done
  16.9 0.1 fusion.29
  17.0 2.2 %collective-permute-start.2 = (f32[2,18,1,256]{3,2,1,0:T(1,128)S(1)}, f32[2,18,1,256]{3,2,1,0:T(1,128)S(1)}, u32[]{:S(2)}, u32[]{:S(2)}) collective-permute-start(f32[2,18,1,256]{3,2,1,0:T(1,128)S(1)} %get-tuple-element.4), channel_id=1, source_target_pairs={{1,0},{2,1},{3,2},{5,4},{6,5},{7,6},{9,8},{10,9},{11,10},{13,12},{... | collective-permute-start | bytes 110600 | tf_op jit(solution)/shard_map/ppermute | solution.py:15
  19.2 3.5 %collective-permute-start.3 = (f32[2,18,1,256]{3,2,1,0:T(1,128)S(1)}, f32[2,18,1,256]{3,2,1,0:T(1,128)}, u32[]{:S(2)}, u32[]{:S(2)}) collective-permute-start(f32[2,18,1,256]{3,2,1,0:T(1,128)S(1)} %get-tuple-element.5), channel_id=1, source_target_pairs={{0,1},{1,2},{2,3},{4,5},{5,6},{6,7},{8,9},{9,10},{10,11},{12,13},{... | collective-permute-start | bytes 110600 | tf_op jit(solution)/shard_map/ppermute | solution.py:14
  22.7 0.1 dynamic-slice_add_fusion
  22.8 0.0 copy-done.7
  22.8 32.6 %scatter_custom_fusion = f32[65536]{0:T(1024)S(1)} fusion(s32[6144]{0:T(1024)S(1)} %bitcast.23, f32[6144]{0:T(1024)S(1)} %bitcast.26, f32[]{:T(128)} %constant.99.clone.1), kind=kCustom, calls=%fused_computation.43 | custom fusion | flops 6144 | bytes 262148 | tf_op jit(solution)/shard_map/scatter-add | solution.py:41
  55.4 0.0 copy-start.3
  55.4 0.1 add.176
  55.5 0.0 collective-permute-done.2
  55.5 0.0 copy-start.5
  55.5 0.6 copy-done.5
  56.1 0.0 collective-permute-done.3
  56.1 0.0 copy-done.4
  56.1 0.2 copy-done.3
  56.3 1.2 %fusion.2 = f32[2,16,16,256]{3,2,1,0:T(8,128)S(1)} fusion(f32[2,16,16,256]{3,2,1,0:T(8,128)S(1)} %copy-done.1, f32[2,18,16,256]{3,2,1,0:T(8,128)S(1)} %constant_dynamic-update-slice_fusion, f32[2,18,1,256]{3,2,1,0:T(1,128)} %collective-permute-done.3, f32[2,18,1,256]{3,2,1,0:T(1,128)} %copy-done.5, f32[2,1,16,256]{3,2,1,0:T(8,128)S(1)} %collective-permute-done.1, ...), kind=kLoop, calls=%fused_computation.11 | loop fusion | flops 2228224 | bytes 2826368 | tf_op jit(solution)/shard_map/add | solution.py:42
  57.6 0.0 copy-start.2
  57.6 1.3 %collective-permute-start.4 = (f32[2,1,16,256]{3,2,1,0:T(8,128)S(1)}, f32[2,1,16,256]{3,2,1,0:T(8,128)S(1)}, u32[]{:S(2)}, u32[]{:S(2)}) collective-permute-start(f32[2,1,16,256]{3,2,1,0:T(8,128)S(1)} %get-tuple-element.7), channel_id=1, source_target_pairs={{4,0},{8,4},{12,8},{5,1},{9,5},{13,9},{6,2},{10,6},{14,10},{7,3},{... | collective-permute-start | bytes 98312 | tf_op jit(solution)/shard_map/ppermute | solution.py:15
  58.9 4.9 %collective-permute-start.5 = (f32[2,1,16,256]{3,2,1,0:T(8,128)S(1)}, f32[2,1,16,256]{3,2,1,0:T(8,128)S(1)}, u32[]{:S(2)}, u32[]{:S(2)}) collective-permute-start(f32[2,1,16,256]{3,2,1,0:T(8,128)S(1)} %get-tuple-element.6), channel_id=1, source_target_pairs={{0,4},{4,8},{8,12},{1,5},{5,9},{9,13},{2,6},{6,10},{10,14},{3,7},{... | collective-permute-start | bytes 98312 | tf_op jit(solution)/shard_map/ppermute | solution.py:14
  63.8 0.0 collective-permute-done.4
  63.8 1.2 %collective-permute-done.5 = f32[2,1,16,256]{3,2,1,0:T(8,128)S(1)} collective-permute-done((f32[2,1,16,256]{3,2,1,0:T(8,128)S(1)}, f32[2,1,16,256]{3,2,1,0:T(8,128)S(1)}, u32[]{:S(2)}, u32[]{:S(2)}) %collective-permute-start.5) | collective-permute-done | bytes 32800 | tf_op jit(solution)/shard_map/ppermute | solution.py:14
  65.0 0.1 pad_maximum_fusion.14
  65.0 2.3 %collective-permute-start.6 = (f32[2,18,1,256]{3,2,1,0:T(1,128)S(1)}, f32[2,18,1,256]{3,2,1,0:T(1,128)S(1)}, u32[]{:S(2)}, u32[]{:S(2)}) collective-permute-start(f32[2,18,1,256]{3,2,1,0:T(1,128)S(1)} %get-tuple-element.2), channel_id=1, source_target_pairs={{1,0},{2,1},{3,2},{5,4},{6,5},{7,6},{9,8},{10,9},{11,10},{13,12},{... | collective-permute-start | bytes 110600 | tf_op jit(solution)/shard_map/ppermute | solution.py:15
  67.3 3.3 %collective-permute-start.7 = (f32[2,18,1,256]{3,2,1,0:T(1,128)S(1)}, f32[2,18,1,256]{3,2,1,0:T(1,128)S(1)}, u32[]{:S(2)}, u32[]{:S(2)}) collective-permute-start(f32[2,18,1,256]{3,2,1,0:T(1,128)S(1)} %get-tuple-element.3), channel_id=1, source_target_pairs={{0,1},{1,2},{2,3},{4,5},{5,6},{6,7},{8,9},{9,10},{10,11},{12,13},{... | collective-permute-start | bytes 110600 | tf_op jit(solution)/shard_map/ppermute | solution.py:14
  70.6 32.8 %scatter_custom_fusion.1 = f32[65536]{0:T(1024)S(1)} fusion(s32[6144]{0:T(1024)} %bitcast.24, f32[6144]{0:T(1024)} %bitcast.25, f32[]{:T(128)} %constant.99.clone.1), kind=kCustom, calls=%fused_computation.41 | custom fusion | flops 6144 | bytes 262656 | tf_op jit(solution)/shard_map/scatter-add | solution.py:41
  103.4 0.1 add.185
  103.5 0.0 collective-permute-done.6
  103.5 0.0 collective-permute-done.7
  103.5 0.0 copy-done.2
  103.5 1.3 %fusion.4 = f32[2,16,16,256]{3,2,1,0:T(8,128)} fusion(f32[2,16,16,256]{3,2,1,0:T(8,128)S(1)} %fusion.2, f32[2,18,1,256]{3,2,1,0:T(1,128)S(1)} %collective-permute-done.7, f32[2,1,16,256]{3,2,1,0:T(8,128)S(1)} %collective-permute-done.4, f32[2,1,16,256]{3,2,1,0:T(8,128)S(1)} %collective-permute-done.5, f32[2,18,1,256]{3,2,1,0:T(1,128)S(1)} %collective-permute-done.6, ...), kind=kLoop, calls=%fused_computation.13 | loop fusion | flops 2752512 | bytes 2236544 | tf_op jit(solution)/shard_map/add | solution.py:42
  (5 shorter events, 0.1 us)
Async XLA Ops:
  0.6 6.9 %copy-start = (f32[2,16,6144]{2,1,0:T(8,128)S(1)}, f32[2,16,6144]{2,1,0:T(8,128)}, u32[]{:S(2)}) copy-start(f32[2,16,6144]{2,1,0:T(8,128)} %param.14) | copy-start | bytes 2359300
  1.5 15.3 %collective-permute-start.1 = (f32[2,1,16,256]{3,2,1,0:T(8,128)S(1)}, f32[2,1,16,256]{3,2,1,0:T(8,128)S(1)}, u32[]{:S(2)}, u32[]{:S(2)}) collective-permute-start(f32[2,1,16,256]{3,2,1,0:T(8,128)S(1)} %get-tuple-element.9), channel_id=1, source_target_pairs={{0,4},{4,8},{8,12},{1,5},{5,9},{9,13},{2,6},{6,10},{10,14},{3,7},{... | collective-permute-start | bytes 98312 | tf_op jit(solution)/shard_map/ppermute | solution.py:14
  5.5 11.4 %collective-permute-start = (f32[2,1,16,256]{3,2,1,0:T(8,128)S(1)}, f32[2,1,16,256]{3,2,1,0:T(8,128)S(1)}, u32[]{:S(2)}, u32[]{:S(2)}) collective-permute-start(f32[2,1,16,256]{3,2,1,0:T(8,128)S(1)} %get-tuple-element.8), channel_id=1, source_target_pairs={{4,0},{8,4},{12,8},{5,1},{9,5},{13,9},{6,2},{10,6},{14,10},{7,3},{... | collective-permute-start | bytes 98312 | tf_op jit(solution)/shard_map/ppermute | solution.py:15
  7.5 0.7 copy-start.8
  8.5 8.3 %copy-start.1 = (f32[2,16,16,256]{3,2,1,0:T(8,128)S(1)}, f32[2,16,16,256]{3,2,1,0:T(8,128)}, u32[]{:S(2)}) copy-start(f32[2,16,16,256]{3,2,1,0:T(8,128)} %param.9) | copy-start | bytes 1572868
  15.1 0.8 copy-start.6
  15.9 0.7 copy-start.9
  15.9 0.7 copy-start.10
  16.6 6.1 %copy-start.7 = (s32[6144,1]{0,1:T(1,128)}, s32[6144,1]{0,1:T(1,128)S(1)}, u32[]{:S(2)}) copy-start(s32[6144,1]{0,1:T(1,128)S(1)} %compare_select_fusion) | copy-start | bytes 73732
  16.9 39.3 %copy-start.4 = (f32[2,16,16,256]{3,2,1,0:T(8,128)S(1)}, f32[2,16,16,256]{3,2,1,0:T(8,128)}, u32[]{:S(2)}) copy-start(f32[2,16,16,256]{3,2,1,0:T(8,128)} %param.10) | copy-start | bytes 1572868
  17.0 38.5 %collective-permute-start.2 = (f32[2,18,1,256]{3,2,1,0:T(1,128)S(1)}, f32[2,18,1,256]{3,2,1,0:T(1,128)S(1)}, u32[]{:S(2)}, u32[]{:S(2)}) collective-permute-start(f32[2,18,1,256]{3,2,1,0:T(1,128)S(1)} %get-tuple-element.4), channel_id=1, source_target_pairs={{1,0},{2,1},{3,2},{5,4},{6,5},{7,6},{9,8},{10,9},{11,10},{13,12},{... | collective-permute-start | bytes 110600 | tf_op jit(solution)/shard_map/ppermute | solution.py:15
  19.2 36.9 %collective-permute-start.3 = (f32[2,18,1,256]{3,2,1,0:T(1,128)S(1)}, f32[2,18,1,256]{3,2,1,0:T(1,128)}, u32[]{:S(2)}, u32[]{:S(2)}) collective-permute-start(f32[2,18,1,256]{3,2,1,0:T(1,128)S(1)} %get-tuple-element.5), channel_id=1, source_target_pairs={{0,1},{1,2},{2,3},{4,5},{5,6},{6,7},{8,9},{9,10},{10,11},{12,13},{... | collective-permute-start | bytes 110600 | tf_op jit(solution)/shard_map/ppermute | solution.py:14
  55.4 1.0 copy-start.3
  55.5 0.6 copy-start.5
  57.6 45.9 %copy-start.2 = (f32[2,16,16,256]{3,2,1,0:T(8,128)}, f32[2,16,16,256]{3,2,1,0:T(8,128)S(1)}, u32[]{:S(2)}) copy-start(f32[2,16,16,256]{3,2,1,0:T(8,128)S(1)} %fusion.2) | copy-start | bytes 1572868
  57.6 6.2 %collective-permute-start.4 = (f32[2,1,16,256]{3,2,1,0:T(8,128)S(1)}, f32[2,1,16,256]{3,2,1,0:T(8,128)S(1)}, u32[]{:S(2)}, u32[]{:S(2)}) collective-permute-start(f32[2,1,16,256]{3,2,1,0:T(8,128)S(1)} %get-tuple-element.7), channel_id=1, source_target_pairs={{4,0},{8,4},{12,8},{5,1},{9,5},{13,9},{6,2},{10,6},{14,10},{7,3},{... | collective-permute-start | bytes 98312 | tf_op jit(solution)/shard_map/ppermute | solution.py:15
  58.9 6.1 %collective-permute-start.5 = (f32[2,1,16,256]{3,2,1,0:T(8,128)S(1)}, f32[2,1,16,256]{3,2,1,0:T(8,128)S(1)}, u32[]{:S(2)}, u32[]{:S(2)}) collective-permute-start(f32[2,1,16,256]{3,2,1,0:T(8,128)S(1)} %get-tuple-element.6), channel_id=1, source_target_pairs={{0,4},{4,8},{8,12},{1,5},{5,9},{9,13},{2,6},{6,10},{10,14},{3,7},{... | collective-permute-start | bytes 98312 | tf_op jit(solution)/shard_map/ppermute | solution.py:14
  65.0 38.4 %collective-permute-start.6 = (f32[2,18,1,256]{3,2,1,0:T(1,128)S(1)}, f32[2,18,1,256]{3,2,1,0:T(1,128)S(1)}, u32[]{:S(2)}, u32[]{:S(2)}) collective-permute-start(f32[2,18,1,256]{3,2,1,0:T(1,128)S(1)} %get-tuple-element.2), channel_id=1, source_target_pairs={{1,0},{2,1},{3,2},{5,4},{6,5},{7,6},{9,8},{10,9},{11,10},{13,12},{... | collective-permute-start | bytes 110600 | tf_op jit(solution)/shard_map/ppermute | solution.py:15
  67.3 36.2 %collective-permute-start.7 = (f32[2,18,1,256]{3,2,1,0:T(1,128)S(1)}, f32[2,18,1,256]{3,2,1,0:T(1,128)S(1)}, u32[]{:S(2)}, u32[]{:S(2)}) collective-permute-start(f32[2,18,1,256]{3,2,1,0:T(1,128)S(1)} %get-tuple-element.3), channel_id=1, source_target_pairs={{0,1},{1,2},{2,3},{4,5},{5,6},{6,7},{8,9},{9,10},{10,11},{12,13},{... | collective-permute-start | bytes 110600 | tf_op jit(solution)/shard_map/ppermute | solution.py:14
